TPU v7x, 256 devices: a whole 4x4x8 slice. The times are simulated.
256 devices in a mesh: cells: 128 (over y_lo, x, z, core), ens: 2 (over y_hi).
Axes of the slice: x: 4, y: 4 (y_hi: 2, y_lo: 2; y = y_hi * 2 + y_lo), z: 8, core: 2. Of those that a mesh axis runs over, the one named last changes fastest.
Arguments:
- later_adjoint: float32 [4, 4, 256, 8, 128], P('ens', None, 'cells'), may hold values from -6 to 6
- coupling: bfloat16 [4, 6, 4, 4, 256, 8, 128], P('ens', None, None, None, 'cells'), may hold values from -0.59765625 to 0.59765625
- diag_inverse: bfloat16 [4, 4, 4, 256, 8, 128], P('ens', None, None, 'cells'), may hold values from -0.7 to 1.6, as said below
- sensitivity: bfloat16 [4, 4, 256, 8, 128, 128], P('ens', None, 'cells'), may hold values from -0.0625 to 0.0625
- well_cells: int32 [256], replicated, may hold values from 0 to 262143
- well_misfit: float32 [4, 4, 256], P('ens'), may hold values from -6 to 6
- block_map: int32 [256, 8, 128], P('cells'), may hold values from 0 to 511, as said below
Outputs:
- adjoint: float32 [4, 4, 256, 8, 128], P('ens', None, 'cells')
- gradient: float32 [512, 128], P('cells')
Inputs may be any that keep to these rules, and one draw needn't show every extreme that they name: `block_map`: of the cells of each slab of 2 planes along the first dimension (x from i * 2 to i * 2 + 1), exactly 16 map to blocks whose number divided by 4 (rounded down) equals any given j. `diag_inverse`: each block is the inverse of a diagonal block; its diagonal entries lie in 0.4 to 1.6. `well_cells`: wells may share a cell.
All inputs are finite; a program needn't handle non-finite values.
Results may differ from a plain program's by a relative error of at most 0.0003.
Values sent between devices are 32-bit elements; how exact they have to be, the bound alone decides.
A program may use at most 64 MiB of HBM per device.

v0:
```python
import jax
import jax.numpy as jnp
from jax import lax
from jax.sharding import PartitionSpec as P

ITERS = 4
BLK_DEV = 4


def from_behind(value, axis, by):
    devices = lax.axis_size(axis)
    pairs = [(i, i + by) for i in range(devices) if 0 <= i + by < devices]
    return lax.ppermute(value, axis, pairs)


def move_along(field, axis, forward):
    length = field.shape[axis]
    shape = list(field.shape)
    shape[axis] = 1
    zeros = jnp.zeros(shape, jnp.float32)
    if forward:
        return jnp.concatenate(
            [zeros, lax.slice_in_dim(field, 0, length - 1, axis=axis)], axis=axis
        )
    return jnp.concatenate([lax.slice_in_dim(field, 1, length, axis=axis), zeros], axis=axis)


def coupling_sum(adjoint, coupling):
    terms = jnp.sum(coupling.astype(jnp.float32) * adjoint[:, None, :, None], axis=2)
    upward = terms[:, 0]
    downward = terms[:, 1]
    planes = upward.shape[2]
    from_below = from_behind(upward[:, :, planes - 1 :], "cells", 1)
    from_above = from_behind(downward[:, :, :1], "cells", -1)
    total = jnp.concatenate([from_below, upward[:, :, : planes - 1]], axis=2)
    total = total + jnp.concatenate([downward[:, :, 1:], from_above], axis=2)
    total = total + move_along(terms[:, 2], 3, True) + move_along(terms[:, 3], 3, False)
    total = total + move_along(terms[:, 4], 4, True) + move_along(terms[:, 5], 4, False)
    return total


def apply_inverse(diag_inverse, source):
    return jnp.sum(diag_inverse.astype(jnp.float32) * source[:, :, None], axis=1)


def body(later_adjoint, coupling, diag_inverse, sensitivity, well_cells, well_misfit, block_map):
    members, unknowns, planes, columns, layers = later_adjoint.shape
    count = planes * columns * layers
    ranks = lax.axis_size("cells")
    first_cell = lax.axis_index("cells") * count
    cell_ids = first_cell + jnp.arange(count, dtype=jnp.int32)
    onehot = (well_cells[:, None] == cell_ids[None, :]).astype(jnp.float32)
    injected = jnp.dot(
        well_misfit.reshape(members * unknowns, -1),
        onehot,
        precision=lax.Precision.HIGHEST,
        preferred_element_type=jnp.float32,
    )
    source = later_adjoint + injected.reshape(later_adjoint.shape)
    adjoint = apply_inverse(diag_inverse, source)
    for sweep in range(ITERS):
        adjoint = apply_inverse(diag_inverse, source - coupling_sum(adjoint, coupling))
    params = sensitivity.shape[-1]
    adjoint_flat = adjoint.reshape(members, unknowns, count)
    sens_flat = sensitivity.reshape(members, unknowns, count, params)
    cell_grad = jnp.sum(adjoint_flat[..., None] * sens_flat.astype(jnp.float32), axis=(0, 1))
    flat_map = block_map.reshape(-1)
    owner = flat_map // BLK_DEV
    order = jnp.argsort(owner, stable=True)
    per_owner = count // ranks
    send_rows = cell_grad[order].reshape(ranks, per_owner, params)
    send_ids = (flat_map[order] % BLK_DEV).astype(jnp.float32).reshape(ranks, per_owner)
    got_rows, got_ids = (
        lax.all_to_all(send_rows, "cells", split_axis=0, concat_axis=0, tiled=True),
        lax.all_to_all(send_ids, "cells", split_axis=0, concat_axis=0, tiled=True),
    )
    owned = jax.ops.segment_sum(
        got_rows.reshape(-1, params), got_ids.reshape(-1).astype(jnp.int32), num_segments=BLK_DEV
    )
    gradient = lax.psum(owned, "ens")
    return (adjoint, gradient)


def solution(mesh):
    placed = (
        P("ens", None, "cells", None, None),
        P("ens", None, None, None, "cells", None, None),
        P("ens", None, None, "cells", None, None),
        P("ens", None, "cells", None, None, None),
        P(),
        P("ens", None, None),
        P("cells", None, None),
    )
    return jax.shard_map(
        body,
        mesh=mesh,
        in_specs=placed,
        out_specs=(P("ens", None, "cells", None, None), P("cells", None)),
        check_vma=False,
    )
```

profile of v0, /device:TPU:1, one launch (start us, length us, event | category | flops | bytes accessed | tf_op | source)
XLA Modules:
  0.0 147.4 jit_solution(6212600087634903519)
XLA Ops:
  0.7 0.8 reshape.110
  1.4 1.4 fusion.6
  2.9 0.9 add.130
  3.7 0.9 fusion.11
  4.9 5.1 %collective-permute-start.1 = (f32[2,4,1,8,128]{4,3,2,1,0:T(8,128)S(1)}, f32[2,4,1,8,128]{4,3,2,1,0:T(8,128)S(1)}, u32[]{:S(2)}, u32[]{:S(2)}) collective-permute-start(f32[2,4,1,8,128]{4,3,2,1,0:T(8,128)S(1)} %get-tuple-element.41), channel_id=1, source_target_pairs={{2,0},{4,2},{6,4},{8,6},{10,8},{12,10},{14,12},{16,14},{18,16},{20... | collective-permute-start | bytes 98312 | tf_op jit(solution)/shard_map/ppermute | solution.py:13
  10.1 1.9 %collective-permute-start = (f32[2,4,1,8,128]{4,3,2,1,0:T(8,128)S(1)}, f32[2,4,1,8,128]{4,3,2,1,0:T(8,128)S(1)}, u32[]{:S(2)}, u32[]{:S(2)}) collective-permute-start(f32[2,4,1,8,128]{4,3,2,1,0:T(8,128)S(1)} %get-tuple-element.42), channel_id=1, source_target_pairs={{0,2},{2,4},{4,6},{6,8},{8,10},{10,12},{12,14},{14,16},{16,18},{18... | collective-permute-start | bytes 98312 | tf_op jit(solution)/shard_map/ppermute | solution.py:13
  12.1 1.1 collective-permute-done
  13.5 2.1 %collective-permute-start.3 = (f32[2,4,1,8,128]{4,3,2,1,0:T(8,128)S(1)}, f32[2,4,1,8,128]{4,3,2,1,0:T(8,128)S(1)}, u32[]{:S(2)}, u32[]{:S(2)}) collective-permute-start(f32[2,4,1,8,128]{4,3,2,1,0:T(8,128)S(1)} %get-tuple-element.37), channel_id=1, source_target_pairs={{2,0},{4,2},{6,4},{8,6},{10,8},{12,10},{14,12},{16,14},{18,16},{20... | collective-permute-start | bytes 98312 | tf_op jit(solution)/shard_map/ppermute | solution.py:13
  15.6 3.9 %collective-permute-start.2 = (f32[2,4,1,8,128]{4,3,2,1,0:T(8,128)S(1)}, f32[2,4,1,8,128]{4,3,2,1,0:T(8,128)S(1)}, u32[]{:S(2)}, u32[]{:S(2)}) collective-permute-start(f32[2,4,1,8,128]{4,3,2,1,0:T(8,128)S(1)} %get-tuple-element.38), channel_id=1, source_target_pairs={{0,2},{2,4},{4,6},{6,8},{8,10},{10,12},{12,14},{14,16},{16,18},{18... | collective-permute-start | bytes 98312 | tf_op jit(solution)/shard_map/ppermute | solution.py:13
  19.6 5.0 %sort.17 = (s32[2048]{0:T(1024)}, s32[2048]{0:T(1024)S(1)}) sort(s32[2048]{0:T(1024)S(1)} %add_select_fusion.1, s32[2048]{0:T(1024)S(1)} %iota.10), dimensions={0}, to_apply=%region_9.0 | sort | flops 22528 | bytes 32768 | tf_op jit(solution)/shard_map/jit(argsort)/sort | solution.py:69
  25.1 1.9 %collective-permute-start.5 = (f32[2,4,1,8,128]{4,3,2,1,0:T(8,128)S(1)}, f32[2,4,1,8,128]{4,3,2,1,0:T(8,128)S(1)}, u32[]{:S(2)}, u32[]{:S(2)}) collective-permute-start(f32[2,4,1,8,128]{4,3,2,1,0:T(8,128)S(1)} %get-tuple-element.33), channel_id=1, source_target_pairs={{2,0},{4,2},{6,4},{8,6},{10,8},{12,10},{14,12},{16,14},{18,16},{20... | collective-permute-start | bytes 98312 | tf_op jit(solution)/shard_map/ppermute | solution.py:13
  27.0 3.6 %collective-permute-start.4 = (f32[2,4,1,8,128]{4,3,2,1,0:T(8,128)S(1)}, f32[2,4,1,8,128]{4,3,2,1,0:T(8,128)S(1)}, u32[]{:S(2)}, u32[]{:S(2)}) collective-permute-start(f32[2,4,1,8,128]{4,3,2,1,0:T(8,128)S(1)} %get-tuple-element.34), channel_id=1, source_target_pairs={{0,2},{2,4},{4,6},{6,8},{8,10},{10,12},{12,14},{14,16},{16,18},{18... | collective-permute-start | bytes 98312 | tf_op jit(solution)/shard_map/ppermute | solution.py:13
  30.7 11.8 %gather_fusion = s32[2048]{0:T(1024)S(1)} fusion(s32[2048]{0:T(1024)S(1)} %bitcast.113, s32[2048]{0:T(1024)S(1)} %fusion.39), kind=kCustom, calls=%fused_computation | custom fusion | bytes 24576 | tf_op jit(solution)/shard_map/gather | solution.py:72
  43.1 1.9 %collective-permute-start.7 = (f32[2,4,1,8,128]{4,3,2,1,0:T(8,128)S(1)}, f32[2,4,1,8,128]{4,3,2,1,0:T(8,128)S(1)}, u32[]{:S(2)}, u32[]{:S(2)}) collective-permute-start(f32[2,4,1,8,128]{4,3,2,1,0:T(8,128)S(1)} %get-tuple-element.29), channel_id=1, source_target_pairs={{2,0},{4,2},{6,4},{8,6},{10,8},{12,10},{14,12},{16,14},{18,16},{20... | collective-permute-start | bytes 98312 | tf_op jit(solution)/shard_map/ppermute | solution.py:13
  45.0 3.6 %collective-permute-start.6 = (f32[2,4,1,8,128]{4,3,2,1,0:T(8,128)S(1)}, f32[2,4,1,8,128]{4,3,2,1,0:T(8,128)S(1)}, u32[]{:S(2)}, u32[]{:S(2)}) collective-permute-start(f32[2,4,1,8,128]{4,3,2,1,0:T(8,128)S(1)} %get-tuple-element.30), channel_id=1, source_target_pairs={{0,2},{2,4},{4,6},{6,8},{8,10},{10,12},{12,14},{14,16},{16,18},{18... | collective-permute-start | bytes 98312 | tf_op jit(solution)/shard_map/ppermute | solution.py:13
  48.7 0.7 copy.59
  49.4 27.0 %all-to-all-start = ((f32[128,1,16]{2,1,0:T(1,128)}), f32[128,1,16]{2,1,0:T(1,128)S(1)}, u32[]{:S(2)}, u32[]{:S(2)}) async-start(f32[128,1,16]{2,1,0:T(1,128)} %copy.59), calls=%async_computation | async-start | bytes 131072 | tf_op jit(solution)/shard_map/all_to_all | solution.py:75
  76.7 4.5 %multiply_reduce_fusion = f32[2,8,128,128]{3,2,1,0:T(8,128)S(1)} fusion(bf16[2,4,2,8,128,128]{5,4,3,2,1,0:T(8,128)(2,1)} %param.10, f32[2,4,2,8,128]{4,3,2,1,0:T(8,128)S(1)} %fusion.15), kind=kLoop, calls=%fused_computation.3 | loop fusion | flops 6029312 | bytes 5308416 | tf_op jit(solution)/shard_map/reduce_sum | solution.py:66
  81.2 7.6 %gather_fusion.1 = f32[2048,128]{1,0:T(8,128)} fusion(f32[2048,128]{1,0:T(8,128)S(1)} %bitcast.114, s32[2048]{0:T(1024)S(1)} %fusion.39), kind=kCustom, calls=%fused_computation.1 | custom fusion | bytes 2105344 | tf_op jit(solution)/shard_map/gather | solution.py:71
  88.8 12.4 %all-to-all-start.1 = ((f32[128,16,128]{2,1,0:T(8,128)}), f32[128,16,128]{2,1,0:T(8,128)S(1)}, u32[]{:S(2)}, u32[]{:S(2)}) async-start(f32[128,16,128]{2,1,0:T(8,128)} %bitcast.27), calls=%async_computation.1 | async-start | bytes 2097152 | tf_op jit(solution)/shard_map/all_to_all | solution.py:74
  101.2 0.2 convert_reduce_fusion
  101.5 28.6 %all-to-all-done.1 = f32[128,16,128]{2,1,0:T(8,128)S(1)} async-done(((f32[128,16,128]{2,1,0:T(8,128)}), f32[128,16,128]{2,1,0:T(8,128)S(1)}, u32[]{:S(2)}, u32[]{:S(2)}) %all-to-all-start.1) | async-done | bytes 1048608 | tf_op jit(solution)/shard_map/all_to_all | solution.py:74
  130.1 11.4 %scatter_custom_fusion = f32[4,128]{1,0:T(4,128)S(1)} fusion(s32[2048]{0:T(1024)S(1)} %reshape.133, f32[2048,128]{1,0:T(8,128)S(1)} %bitcast.115, f32[]{:T(128)} %constant.36.clone.1), kind=kCustom, calls=%fused_computation.91 | custom fusion | flops 262144 | bytes 2052 | tf_op jit(solution)/shard_map/scatter-add | solution.py:77
  141.5 5.9 %psum.7 = f32[4,128]{1,0:T(4,128)} all-reduce(f32[4,128]{1,0:T(4,128)S(1)} %scatter_custom_fusion), channel_id=1, replica_groups=mesh['cells'=128,'ens'=2] {'ens'}, use_global_device_ids=true, to_apply=%region_12.13 | all-reduce | flops 512 | bytes 4096 | tf_op jit(solution)/shard_map/psum | solution.py:80
  (57 shorter events, 2.0 us)
Async XLA Ops:
  0.6 4.1 %copy-start.1 = (bf16[2,6,4,4,2,8,128]{6,5,4,3,2,1,0:T(8,128)(2,1)S(1)}, bf16[2,6,4,4,2,8,128]{6,5,4,3,2,1,0:T(8,128)(2,1)}, u32[]{:S(2)}) copy-start(bf16[2,6,4,4,2,8,128]{6,5,4,3,2,1,0:T(8,128)(2,1)} %param.8) | copy-start | bytes 2359300
  4.7 8.6 %copy-start.2 = (bf16[2,4,4,2,8,128]{5,4,3,2,1,0:T(8,128)(2,1)S(1)}, bf16[2,4,4,2,8,128]{5,4,3,2,1,0:T(8,128)(2,1)}, u32[]{:S(2)}) copy-start(bf16[2,4,4,2,8,128]{5,4,3,2,1,0:T(8,128)(2,1)} %param.9) | copy-start | bytes 393220
  4.9 7.2 %collective-permute-start.1 = (f32[2,4,1,8,128]{4,3,2,1,0:T(8,128)S(1)}, f32[2,4,1,8,128]{4,3,2,1,0:T(8,128)S(1)}, u32[]{:S(2)}, u32[]{:S(2)}) collective-permute-start(f32[2,4,1,8,128]{4,3,2,1,0:T(8,128)S(1)} %get-tuple-element.41), channel_id=1, source_target_pairs={{2,0},{4,2},{6,4},{8,6},{10,8},{12,10},{14,12},{16,14},{18,16},{20... | collective-permute-start | bytes 98312 | tf_op jit(solution)/shard_map/ppermute | solution.py:13
  10.1 3.1 %collective-permute-start = (f32[2,4,1,8,128]{4,3,2,1,0:T(8,128)S(1)}, f32[2,4,1,8,128]{4,3,2,1,0:T(8,128)S(1)}, u32[]{:S(2)}, u32[]{:S(2)}) collective-permute-start(f32[2,4,1,8,128]{4,3,2,1,0:T(8,128)S(1)} %get-tuple-element.42), channel_id=1, source_target_pairs={{0,2},{2,4},{4,6},{6,8},{8,10},{10,12},{12,14},{14,16},{16,18},{18... | collective-permute-start | bytes 98312 | tf_op jit(solution)/shard_map/ppermute | solution.py:13
  12.1 7.4 %copy-start = (s32[2,8,128]{2,1,0:T(8,128)S(1)}, s32[2,8,128]{2,1,0:T(8,128)}, u32[]{:S(2)}) copy-start(s32[2,8,128]{2,1,0:T(8,128)} %param.13) | copy-start | bytes 24580
  13.5 11.2 %collective-permute-start.3 = (f32[2,4,1,8,128]{4,3,2,1,0:T(8,128)S(1)}, f32[2,4,1,8,128]{4,3,2,1,0:T(8,128)S(1)}, u32[]{:S(2)}, u32[]{:S(2)}) collective-permute-start(f32[2,4,1,8,128]{4,3,2,1,0:T(8,128)S(1)} %get-tuple-element.37), channel_id=1, source_target_pairs={{2,0},{4,2},{6,4},{8,6},{10,8},{12,10},{14,12},{16,14},{18,16},{20... | collective-permute-start | bytes 98312 | tf_op jit(solution)/shard_map/ppermute | solution.py:13
  15.6 9.1 %collective-permute-start.2 = (f32[2,4,1,8,128]{4,3,2,1,0:T(8,128)S(1)}, f32[2,4,1,8,128]{4,3,2,1,0:T(8,128)S(1)}, u32[]{:S(2)}, u32[]{:S(2)}) collective-permute-start(f32[2,4,1,8,128]{4,3,2,1,0:T(8,128)S(1)} %get-tuple-element.38), channel_id=1, source_target_pairs={{0,2},{2,4},{4,6},{6,8},{8,10},{10,12},{12,14},{14,16},{16,18},{18... | collective-permute-start | bytes 98312 | tf_op jit(solution)/shard_map/ppermute | solution.py:13
  25.1 17.6 %collective-permute-start.5 = (f32[2,4,1,8,128]{4,3,2,1,0:T(8,128)S(1)}, f32[2,4,1,8,128]{4,3,2,1,0:T(8,128)S(1)}, u32[]{:S(2)}, u32[]{:S(2)}) collective-permute-start(f32[2,4,1,8,128]{4,3,2,1,0:T(8,128)S(1)} %get-tuple-element.33), channel_id=1, source_target_pairs={{2,0},{4,2},{6,4},{8,6},{10,8},{12,10},{14,12},{16,14},{18,16},{20... | collective-permute-start | bytes 98312 | tf_op jit(solution)/shard_map/ppermute | solution.py:13
  27.0 15.7 %collective-permute-start.4 = (f32[2,4,1,8,128]{4,3,2,1,0:T(8,128)S(1)}, f32[2,4,1,8,128]{4,3,2,1,0:T(8,128)S(1)}, u32[]{:S(2)}, u32[]{:S(2)}) collective-permute-start(f32[2,4,1,8,128]{4,3,2,1,0:T(8,128)S(1)} %get-tuple-element.34), channel_id=1, source_target_pairs={{0,2},{2,4},{4,6},{6,8},{8,10},{10,12},{12,14},{14,16},{16,18},{18... | collective-permute-start | bytes 98312 | tf_op jit(solution)/shard_map/ppermute | solution.py:13
  43.1 33.4 %collective-permute-start.7 = (f32[2,4,1,8,128]{4,3,2,1,0:T(8,128)S(1)}, f32[2,4,1,8,128]{4,3,2,1,0:T(8,128)S(1)}, u32[]{:S(2)}, u32[]{:S(2)}) collective-permute-start(f32[2,4,1,8,128]{4,3,2,1,0:T(8,128)S(1)} %get-tuple-element.29), channel_id=1, source_target_pairs={{2,0},{4,2},{6,4},{8,6},{10,8},{12,10},{14,12},{16,14},{18,16},{20... | collective-permute-start | bytes 98312 | tf_op jit(solution)/shard_map/ppermute | solution.py:13
  45.0 31.5 %collective-permute-start.6 = (f32[2,4,1,8,128]{4,3,2,1,0:T(8,128)S(1)}, f32[2,4,1,8,128]{4,3,2,1,0:T(8,128)S(1)}, u32[]{:S(2)}, u32[]{:S(2)}) collective-permute-start(f32[2,4,1,8,128]{4,3,2,1,0:T(8,128)S(1)} %get-tuple-element.30), channel_id=1, source_target_pairs={{0,2},{2,4},{4,6},{6,8},{8,10},{10,12},{12,14},{14,16},{16,18},{18... | collective-permute-start | bytes 98312 | tf_op jit(solution)/shard_map/ppermute | solution.py:13
  49.4 39.4 %all-to-all-start = ((f32[128,1,16]{2,1,0:T(1,128)}), f32[128,1,16]{2,1,0:T(1,128)S(1)}, u32[]{:S(2)}, u32[]{:S(2)}) async-start(f32[128,1,16]{2,1,0:T(1,128)} %copy.59), calls=%async_computation | async-start | bytes 131072 | tf_op jit(solution)/shard_map/all_to_all | solution.py:75
  76.7 4.5 %copy-start.3 = (f32[2,4,2,8,128]{4,3,2,1,0:T(8,128)}, f32[2,4,2,8,128]{4,3,2,1,0:T(8,128)S(1)}, u32[]{:S(2)}) copy-start(f32[2,4,2,8,128]{4,3,2,1,0:T(8,128)S(1)} %fusion.15) | copy-start | bytes 196612
  88.8 41.3 %all-to-all-start.1 = ((f32[128,16,128]{2,1,0:T(8,128)}), f32[128,16,128]{2,1,0:T(8,128)S(1)}, u32[]{:S(2)}, u32[]{:S(2)}) async-start(f32[128,16,128]{2,1,0:T(8,128)} %bitcast.27), calls=%async_computation.1 | async-start | bytes 2097152 | tf_op jit(solution)/shard_map/all_to_all | solution.py:74
where the time goes:
time: 149 us; the launch traced here: 147 us
  starting transfers between devices  63.6 us (43%)
  waiting for transfers between devices  29.7 us (20%)
  other arithmetic  24.1 us (16%)
  local copies, waits for them, and re-layouts  21.6 us (14%)
  blocking collectives  5.85 us (4%)
    all_to_all x1, waiting for transfers between devices, body(): lax.all_to_all(send_rows, 'cells', split_axis=0, concat_axis=0, tiled=True)  28.6 us
    all_to_all x1, starting transfers between devices, body(): lax.all_to_all(send_ids, 'cells', split_axis=0, concat_axis=0, tiled=True)  27 us
    ppermute x8, starting transfers between devices, from_behind(): return lax.ppermute(value, axis, pairs)  24.1 us
    all_to_all x1, starting transfers between devices, body(): lax.all_to_all(send_rows, 'cells', split_axis=0, concat_axis=0, tiled=True)  12.4 us
    gather x3, local copies, waits for them, and re-layouts, body(): flat_map[order] % BLK_DEV  11.9 us
    scatter-add x1, other arithmetic, body(): jax.ops.segment_sum(got_rows.reshape(-1, params), got_ids.reshape(-1).ast...  11.4 us
    gather x1, local copies, waits for them, and re-layouts, body(): send_rows = cell_grad[order].reshape(ranks, per_owner, params)  7.58 us
    psum x1, blocking collectives, body(): gradient = lax.psum(owned, 'ens')  5.85 us
  transfers between devices with their start and end apart: 10, of which 2 were waited for; matrix products, arithmetic and copies ran while one was open for 21% of the time, Pallas kernels for 0%

commit v1 on v0

v1 whole, which is shorter than its diff:
```python
import jax
import jax.numpy as jnp
from jax import lax
from jax.experimental import pallas as pl
from jax.experimental.pallas import tpu as pltpu
from jax.sharding import PartitionSpec as P

ITERS = 4
MESH = pl.DeviceIdType.MESH
F32 = jnp.float32
BF16 = jnp.bfloat16


def kernel(
    later_hbm, coup_hbm, dinv_hbm, sens_hbm, well_hbm, misfit_hbm, map_hbm,
    adj_ref, grad_ref,
    later, coup, dinv, sens, well, misfit, bmap,
    onehot, rhs, total, got, mine, arrived,
    halo_out, halo_in, load_sem,
    halo_send, halo_recv, send1, recv1, send2, recv2,
):
    cell = lax.axis_index("cells")
    ens = lax.axis_index("ens")
    last = lax.axis_size("cells") - 1
    core = cell % 2
    z = (cell // 2) % 8
    x = (cell // 16) % 4
    y = cell // 64

    def first_peer(step):
        dy, dx, dc = step // 8, (step // 2) % 4, step % 2
        py, px, pc = (y + dy) % 2, (x + dx) % 4, (core + dc) % 2
        return (py * 4 + px) * 16 + z * 2 + pc, (py * 4 + px) * 2 + pc

    def second_peer(step):
        de, dz = step // 8, step % 8
        pe, pz = (ens + de) % 2, (z + dz) % 8
        return pe, cell - z * 2 + pz * 2, pz, pe * 8 + pz

    barrier = pltpu.get_barrier_semaphore()
    has_below = cell > 0
    has_above = cell < last

    @pl.when(has_below)
    def _():
        pl.semaphore_signal(barrier, inc=1, device_id={"cells": cell - 1}, device_id_type=MESH)

    @pl.when(has_above)
    def _():
        pl.semaphore_signal(barrier, inc=1, device_id={"cells": cell + 1}, device_id_type=MESH)

    for step in range(1, 16):
        pl.semaphore_signal(barrier, inc=1, device_id={"cells": first_peer(step)[0]}, device_id_type=MESH)
        pe, pc, _, _ = second_peer(step)
        pl.semaphore_signal(barrier, inc=1, device_id={"cells": pc, "ens": pe}, device_id_type=MESH)

    loads = [
        pltpu.make_async_copy(src, dst, load_sem.at[i])
        for i, (src, dst) in enumerate([
            (well_hbm, well), (misfit_hbm, misfit), (later_hbm, later), (dinv_hbm, dinv),
            (coup_hbm, coup), (map_hbm, bmap), (sens_hbm, sens),
        ])
    ]
    for load in loads:
        load.start()

    for load in loads[:4]:
        load.wait()
    slot = jnp.concatenate([well[0:1], well[1:2]], axis=1) - cell * 2048
    row = slot // 128
    inside = (slot >= 0) & (slot < 2048)
    hit_xy = (jnp.where(inside, row, -1) == lax.broadcasted_iota(jnp.int32, (16, 256), 0))
    hit_z = (slot - row * 128 == lax.broadcasted_iota(jnp.int32, (128, 256), 0))
    hit_z = jnp.where(hit_z, 1.0, 0.0).astype(BF16)
    spread = jnp.concatenate(
        [jnp.where(hit_xy, jnp.broadcast_to(misfit[m, u : u + 1], (16, 256)), 0.0) for m in range(2) for u in range(4)],
        axis=0,
    )
    injected = jnp.zeros((128, 128), F32)
    for _ in range(3):
        part = spread.astype(BF16)
        injected = injected + lax.dot_general(part, hit_z, (((1,), (1,)), ((), ())), preferred_element_type=F32)
        spread = spread - part.astype(F32)
    source = later[...] + injected.reshape(2, 4, 2, 8, 128)

    def apply_inverse(field):
        return jnp.sum(dinv[...].astype(F32) * field[:, :, None], axis=1)

    lane = lax.broadcasted_iota(jnp.int32, (16, 8, 128), 2)
    sub = lax.broadcasted_iota(jnp.int32, (16, 8, 128), 1)

    def shifted(field, axis, forward):
        flat = field.reshape(16, 8, 128)
        length = flat.shape[axis]
        index = sub if axis == 1 else lane
        moved = pltpu.roll(flat, 1 if forward else length - 1, axis)
        return jnp.where(index == (0 if forward else length - 1), 0.0, moved).reshape(field.shape)

    def products(k, adjoint):
        return jnp.sum(coup[:, k].astype(F32) * adjoint[:, :, None], axis=1)

    adjoint = apply_inverse(source)
    loads[4].wait()
    pl.semaphore_wait(barrier, 30 + has_below.astype(jnp.int32) + has_above.astype(jnp.int32))

    @pl.when(jnp.logical_not(has_below))
    def _():
        halo_in[:, 0] = jnp.zeros(halo_in[:, 0].shape, F32)

    @pl.when(jnp.logical_not(has_above))
    def _():
        halo_in[:, 1] = jnp.zeros(halo_in[:, 1].shape, F32)

    def halo_copies(sweep):
        up = pltpu.make_async_remote_copy(
            src_ref=halo_out.at[sweep, 0], dst_ref=halo_in.at[sweep, 0],
            send_sem=halo_send.at[sweep, 0], recv_sem=halo_recv.at[sweep, 0],
            device_id={"cells": jnp.minimum(cell + 1, last)}, device_id_type=MESH,
        )
        down = pltpu.make_async_remote_copy(
            src_ref=halo_out.at[sweep, 1], dst_ref=halo_in.at[sweep, 1],
            send_sem=halo_send.at[sweep, 1], recv_sem=halo_recv.at[sweep, 1],
            device_id={"cells": jnp.maximum(cell - 1, 0)}, device_id_type=MESH,
        )
        return up, down

    for sweep in range(ITERS):
        upward = products(0, adjoint)
        downward = products(1, adjoint)
        halo_out[sweep, 0] = upward[:, :, 1]
        halo_out[sweep, 1] = downward[:, :, 0]
        up, down = halo_copies(sweep)

        @pl.when(has_above)
        def _():
            up.start()

        @pl.when(has_below)
        def _():
            down.start()

        field = source
        field = field - shifted(products(2, adjoint), 1, True)
        field = field - shifted(products(3, adjoint), 1, False)
        field = field - shifted(products(4, adjoint), 2, True)
        field = field - shifted(products(5, adjoint), 2, False)
        if sweep == 0:
            loads[5].wait()
            block = bmap[...]
            place = (block // 64) * 64 + ((block // 4) % 2) * 32 + ((block // 8) % 8) * 4 + block % 4
            rows = lax.broadcasted_iota(jnp.int32, (512, 128), 0)
            for i in range(16):
                hit = jnp.broadcast_to(place[i // 8, i % 8][None, :], (512, 128)) == rows
                onehot[:, i * 128 : (i + 1) * 128] = jnp.where(hit, 1.0, 0.0).astype(BF16)

        @pl.when(has_below)
        def _():
            up.wait_recv()

        @pl.when(has_above)
        def _():
            down.wait_recv()

        low = field[:, :, 0] - downward[:, :, 1] - halo_in[sweep, 0]
        high = field[:, :, 1] - upward[:, :, 0] - halo_in[sweep, 1]
        adjoint = apply_inverse(jnp.stack([low, high], axis=2))

    adj_ref[...] = adjoint

    loads[6].wait()
    columns = [adjoint[m, u].reshape(16, 128).T for m in range(2) for u in range(4)]
    for i in range(16):
        cell_grad = jnp.zeros((128, 128), F32)
        for m in range(2):
            for u in range(4):
                cell_grad = cell_grad + columns[m * 4 + u][:, i : i + 1] * sens[m, u, i // 8, i % 8].astype(F32)
        high = cell_grad.astype(BF16)
        rhs[i * 128 : (i + 1) * 128, :128] = high
        rhs[i * 128 : (i + 1) * 128, 128:] = (cell_grad - high.astype(F32)).astype(BF16)
    both = jnp.dot(onehot[...], rhs[...], preferred_element_type=F32)
    total[...] = (both[:, :128] + both[:, 128:]).reshape(16, 32, 128)

    copies = []
    for step in range(1, 16):
        peer, piece = first_peer(step)
        copies.append(pltpu.make_async_remote_copy(
            src_ref=total.at[piece], dst_ref=got.at[step],
            send_sem=send1.at[step], recv_sem=recv1.at[step],
            device_id={"cells": peer}, device_id_type=MESH,
        ))
    for copy in copies:
        copy.start()
    partial = total[(y * 4 + x) * 2 + core]
    for step in range(1, 16):
        copies[step - 1].wait_recv()
        partial = partial + got[step]
    mine[...] = partial.reshape(8, 4, 128)

    own = ens * 8 + z
    later_copies = []
    for step in range(1, 16):
        pe, pc, pz, slot_of = second_peer(step)
        later_copies.append((pltpu.make_async_remote_copy(
            src_ref=mine.at[pz], dst_ref=arrived.at[own],
            send_sem=send2.at[step], recv_sem=recv2.at[own],
            device_id={"cells": pc, "ens": pe}, device_id_type=MESH,
        ), slot_of))
    for copy, _ in later_copies:
        copy.start()
    arrived[own] = mine[z]
    for copy, slot_of in later_copies:
        pltpu.make_async_remote_copy(
            src_ref=mine.at[0], dst_ref=arrived.at[slot_of],
            send_sem=send2.at[0], recv_sem=recv2.at[slot_of],
            device_id={"cells": cell}, device_id_type=MESH,
        ).wait_recv()
    gradient = arrived[0]
    for i in range(1, 16):
        gradient = gradient + arrived[i]
    grad_ref[...] = gradient

    for sweep in range(ITERS):
        up, down = halo_copies(sweep)

        @pl.when(has_above)
        def _():
            up.wait_send()

        @pl.when(has_below)
        def _():
            down.wait_send()

    for copy in copies:
        copy.wait_send()
    for copy, _ in later_copies:
        copy.wait_send()


def body(later_adjoint, coupling, diag_inverse, sensitivity, well_cells, well_misfit, block_map):
    any_spec = pl.BlockSpec(memory_space=pl.ANY)
    vmem = pl.BlockSpec(memory_space=pltpu.VMEM)
    args = (later_adjoint, coupling, diag_inverse, sensitivity, well_cells.reshape(2, 128), well_misfit, block_map)
    dma = pltpu.SemaphoreType.DMA
    return pl.pallas_call(
        kernel,
        out_shape=(
            jax.ShapeDtypeStruct(later_adjoint.shape, F32),
            jax.ShapeDtypeStruct((4, 128), F32),
        ),
        in_specs=[any_spec] * 7,
        out_specs=(vmem, vmem),
        scratch_shapes=[pltpu.VMEM(a.shape, a.dtype) for a in args] + [
            pltpu.VMEM((512, 2048), BF16),
            pltpu.VMEM((2048, 256), BF16),
            pltpu.VMEM((16, 32, 128), F32),
            pltpu.VMEM((16, 32, 128), F32),
            pltpu.VMEM((8, 4, 128), F32),
            pltpu.VMEM((16, 4, 128), F32),
            pltpu.VMEM((ITERS, 2, 2, 4, 8, 128), F32),
            pltpu.VMEM((ITERS, 2, 2, 4, 8, 128), F32),
            dma((7,)),
            dma((ITERS, 2)), dma((ITERS, 2)),
            dma((16,)), dma((16,)), dma((16,)), dma((16,)),
        ],
        compiler_params=pltpu.CompilerParams(collective_id=0, has_side_effects=True),
        name="adjoint_step",
    )(*args)


def solution(mesh):
    placed = (
        P("ens", None, "cells", None, None),
        P("ens", None, None, None, "cells", None, None),
        P("ens", None, None, "cells", None, None),
        P("ens", None, "cells", None, None, None),
        P(),
        P("ens", None, None),
        P("cells", None, None),
    )
    return jax.shard_map(
        body,
        mesh=mesh,
        in_specs=placed,
        out_specs=(P("ens", None, "cells", None, None), P("cells", None)),
        check_vma=False,
    )
```

time: 149 us -> 44 us (0.30)
  starting transfers between devices: 63.6 us -> 0 us
  Pallas kernels: 0 us -> 40.2 us
  waiting for transfers between devices: 29.7 us -> 0 us
  other arithmetic: 24.1 us -> 0 us
  local copies, waits for them, and re-layouts: 21.6 us -> 2.72 us
  blocking collectives: 5.85 us -> 0 us
    pallas_call x0 -> x1, Pallas kernels: none -> 40.2 us  [body(): pl.pallas_call(kernel, out_shape=(jax.ShapeDtypeStruct(later_adjoint.shap...]
    all_to_all x2 -> x0, starting transfers between devices: 39.5 us -> none  [the longest x1 27 us: body(): lax.all_to_all(send_ids, 'cells', split_axis=0, concat_axis=0, tiled=True)]
    all_to_all x2 -> x0, waiting for transfers between devices: 28.6 us -> none  [the longest x1 28.6 us: body(): lax.all_to_all(send_rows, 'cells', split_axis=0, concat_axis=0, tiled=True)]
    ppermute x8 -> x0, starting transfers between devices: 24.1 us -> none  [from_behind(): return lax.ppermute(value, axis, pairs)]
    gather x4 -> x0, local copies, waits for them, and re-layouts: 19.5 us -> none  [the longest x3 11.9 us: body(): flat_map[order] % BLK_DEV]
    scatter-add x1 -> x0, other arithmetic: 11.4 us -> none  [body(): jax.ops.segment_sum(got_rows.reshape(-1, params), got_ids.reshape(-1).ast...]
    reduce_sum x10 -> x0, other arithmetic: 6.21 us -> none  [the longest x1 4.47 us: body(): jnp.sum(adjoint_flat[..., None] * sens_flat.astype(jnp.float32), axis=(0,...]
    psum x1 -> x0, blocking collectives: 5.85 us -> none  [body(): gradient = lax.psum(owned, 'ens')]
  transfers between devices with their start and end apart: 10 -> 0, of which waited for: 2 -> 0; matrix products, arithmetic and copies ran while one was open for 21% -> 0% of each run, Pallas kernels for 0% -> 0%
where the time goes in v1:
time: 44 us; the launch traced here: 43.6 us
  Pallas kernels  40.2 us (91%)
  local copies, waits for them, and re-layouts  2.72 us (6%)
  between operations  0.64 us (1%)
    pallas_call x1, Pallas kernels, body(): pl.pallas_call(kernel, out_shape=(jax.ShapeDtypeStruct(later_adjoint.shap...  40.2 us
    unnamed x2, local copies, waits for them, and re-layouts  2.72 us

profile of v1, /device:TPU:1, one launch (start us, length us, event | category | flops | bytes accessed | tf_op | source)
XLA Modules:
  0.0 43.6 jit_solution(5847904016352708669)
XLA Ops:
  0.6 40.2 %adjoint_step.1 = (f32[2,4,2,8,128]{4,3,2,1,0:T(8,128)}, f32[4,128]{1,0:T(4,128)}) custom-call(f32[2,4,2,8,128]{4,3,2,1,0:T(8,128)} %later_hbm.1, bf16[2,6,4,4,2,8,128]{6,5,4,3,2,1,0:T(8,128)(2,1)} %coup_hbm.1, bf16[2,4,4,2,8,128]{5,4,3,2,1,0:T(8,128)(2,1)} %dinv_hbm.1, bf16[2,4,2,8,128,128]{5,4,3,2,1,0:T(8,128)(2,1)} %sens_hbm.1, s32[2,128]{1,0:T(2,128)} %bitcast.1, ...), custom_call_target="tpu_custom_call" | custom-call | tf_op jit(solution)/shard_map/adjoint_step/pallas_call | solution.py:244
  40.9 1.5 %copy.11 = f32[2,4,2,8,128]{4,3,2,1,0:T(8,128)} copy(f32[2,4,2,8,128]{4,3,2,1,0:T(8,128)} %get-tuple-element.4) | data formatting | bytes 131072
  42.4 1.2 %copy.12 = f32[4,128]{1,0:T(4,128)} copy(f32[4,128]{1,0:T(4,128)} %get-tuple-element.5) | data formatting | bytes 4096

commit v2 on v1

v2 whole, which is shorter than its diff:
```python
import jax
import jax.numpy as jnp
from jax import lax
from jax.experimental import pallas as pl
from jax.experimental.pallas import tpu as pltpu
from jax.sharding import PartitionSpec as P

MESH = pl.DeviceIdType.MESH
F32 = jnp.float32
BF16 = jnp.bfloat16
INT = jnp.int32


def kernel(
    later_hbm, coup_hbm, dinv_hbm, sens_hbm, well_hbm, misfit_hbm, map_hbm,
    adj_ref, grad_ref,
    later, coup, dinv, sens, well, misfit, bmap,
    turned, onehot, rhs, total, core_in, mixed, got, mine, arrived,
    edge_out, edge_in,
    load_sem, edge_sem, core_sem, first_sem, second_sem, token,
):
    cell = lax.axis_index("cells")
    ens = lax.axis_index("ens")
    last = lax.axis_size("cells") - 1
    core = cell % 2
    z = (cell // 2) % 8
    x = (cell // 16) % 4
    y = cell // 64

    def first_peer(step):
        return (((y + step // 4) % 2) * 4 + (x + step % 4) % 4) * 16 + z * 2 + core

    def along_z(by):
        return cell - z * 2 + ((z + by + 8) % 8) * 2

    def remote(src, dst, send, recv, **where):
        return pltpu.make_async_remote_copy(
            src_ref=src, dst_ref=dst, send_sem=send, recv_sem=recv, device_id=where, device_id_type=MESH,
        )

    def await_bytes(ref, sem):
        pltpu.make_async_copy(ref, ref, sem).wait()

    def signal(sem, **where):
        pl.semaphore_signal(sem, inc=1, device_id=where, device_id_type=MESH)

    barrier = pltpu.get_barrier_semaphore()
    has_below = cell > 0
    has_above = cell < last

    @pl.when(has_below)
    def _():
        signal(barrier, cells=cell - 1)

    @pl.when(has_above)
    def _():
        signal(barrier, cells=cell + 1)

    loads = [
        pltpu.make_async_copy(src, dst, load_sem.at[i])
        for i, (src, dst) in enumerate([
            (well_hbm, well), (misfit_hbm, misfit), (later_hbm, later), (dinv_hbm, dinv),
            (coup_hbm, coup), (map_hbm, bmap), (sens_hbm, sens),
        ])
    ]
    for load in loads:
        load.start()
    for step in range(1, 8):
        signal(barrier, cells=first_peer(step))
    signal(barrier, ens=1 - ens)
    signal(barrier, cells=along_z(1))
    signal(barrier, cells=along_z(-1))
    for load in loads[:4]:
        load.wait()
    slot = jnp.concatenate([well[0:1], well[1:2]], axis=1) - cell * 2048
    row = slot // 128
    inside = (slot >= 0) & (slot < 2048)
    hit_xy = (jnp.where(inside, row, -1) == lax.broadcasted_iota(INT, (16, 256), 0))
    hit_z = (slot - row * 128 == lax.broadcasted_iota(INT, (128, 256), 0))
    hit_z = jnp.where(hit_z, 1.0, 0.0).astype(BF16)
    spread = jnp.concatenate(
        [jnp.where(hit_xy, jnp.broadcast_to(misfit[m, u : u + 1], (16, 256)), 0.0) for m in range(2) for u in range(4)],
        axis=0,
    )
    injected = jnp.zeros((128, 128), F32)
    for _ in range(3):
        part = spread.astype(BF16)
        injected = injected + lax.dot_general(part, hit_z, (((1,), (1,)), ((), ())), preferred_element_type=F32)
        spread = spread - part.astype(F32)
    source = later[...] + injected.reshape(2, 4, 2, 8, 128)

    def apply_inverse(field):
        return jnp.sum(dinv[...].astype(F32) * field[:, :, None], axis=1)

    lane = lax.broadcasted_iota(INT, (16, 8, 128), 2)
    sub = lax.broadcasted_iota(INT, (16, 8, 128), 1)

    def shifted(field, axis, forward):
        flat = field.reshape(16, 8, 128)
        length = flat.shape[axis]
        index = sub if axis == 1 else lane
        moved = pltpu.roll(flat, 1 if forward else length - 1, axis)
        return jnp.where(index == (0 if forward else length - 1), 0.0, moved).reshape(field.shape)

    def products(k, adjoint):
        return jnp.sum(coup[:, k].astype(F32) * adjoint[:, :, None], axis=1)

    def plane_products(k, plane, values):
        return jnp.sum(coup[:, k, :, :, plane].astype(F32) * values[:, :, None], axis=1)

    def without_halo(adjoint):
        field = source
        field = field - shifted(products(2, adjoint), 1, True)
        field = field - shifted(products(3, adjoint), 1, False)
        field = field - shifted(products(4, adjoint), 2, True)
        field = field - shifted(products(5, adjoint), 2, False)
        return take_off(field, plane_products(1, 1, adjoint[:, :, 1]), plane_products(0, 0, adjoint[:, :, 0]))

    def take_off(field, low, high):
        return jnp.stack([field[:, :, 0] - low, field[:, :, 1] - high], axis=2)

    adjoint = apply_inverse(source)
    loads[4].wait()
    for side, (k, plane) in enumerate([(0, 1), (1, 0)]):
        for w in range(4):
            edge_out[side, 2 + w] = jnp.sum(
                dinv[:, w, :, plane].astype(F32)[:, :, None] * coup[:, k, :, :, plane].astype(F32), axis=1
            )
    pl.semaphore_wait(barrier, 10 + has_below.astype(INT) + has_above.astype(INT))
    signal(token.at[0], cells=along_z(1))
    signal(token.at[0], cells=along_z(-1))

    @pl.when(jnp.logical_not(has_below))
    def _():
        edge_in[0] = jnp.zeros(edge_in[0].shape, F32)

    @pl.when(jnp.logical_not(has_above))
    def _():
        edge_in[1] = jnp.zeros(edge_in[1].shape, F32)

    def send_edges(slots, sem):
        @pl.when(has_above)
        def _():
            remote(edge_out.at[0, slots], edge_in.at[0, slots], load_sem.at[0], edge_sem.at[0, sem], cells=jnp.minimum(cell + 1, last)).start()

        @pl.when(has_below)
        def _():
            remote(edge_out.at[1, slots], edge_in.at[1, slots], load_sem.at[1], edge_sem.at[1, sem], cells=jnp.maximum(cell - 1, 0)).start()

    def await_edges(slots, sem):
        @pl.when(has_below)
        def _():
            await_bytes(edge_in.at[0, slots], edge_sem.at[0, sem])

        @pl.when(has_above)
        def _():
            await_bytes(edge_in.at[1, slots], edge_sem.at[1, sem])

    for turn in range(2):
        at = turn * 6
        upward = plane_products(0, 1, adjoint[:, :, 1])
        downward = plane_products(1, 0, adjoint[:, :, 0])
        edge_out[0, at] = upward
        edge_out[1, at] = downward
        send_edges(pl.ds(at, 1), turn * 2)
        if turn == 0:
            send_edges(pl.ds(2, 4), 1)
        field = without_halo(adjoint)
        alone = apply_inverse(field)
        edge_out[0, at + 1] = plane_products(0, 1, alone[:, :, 1])
        edge_out[1, at + 1] = plane_products(1, 0, alone[:, :, 0])
        send_edges(pl.ds(at + 1, 1), turn * 2 + 1)
        if turn == 0:
            loads[5].wait()
            block = bmap[...]
            place = (
                (((block // 4) % 2 + core) % 2) * 256
                + ((block // 256 + y) % 2) * 128
                + (((block // 64) % 4 - x + 4) % 4) * 32
                + (((block // 8) % 8 - z + 14) % 8) * 4
                + block % 4
            )
            rows = lax.broadcasted_iota(INT, (512, 128), 0)
            for i in range(16):
                hit = jnp.broadcast_to(place[i // 8, i % 8][None, :], (512, 128)) == rows
                onehot[:, i * 128 : (i + 1) * 128] = jnp.where(hit, 1.0, 0.0).astype(BF16)
            loads[6].wait()

            def turn_over(i, carry):
                for mu in range(8):
                    turned[mu, i] = sens[mu, i].T
                return carry

            lax.fori_loop(0, 16, turn_over, 0, unroll=4)
        await_edges(pl.ds(at, 1), turn * 2)
        adjoint = apply_inverse(take_off(field, edge_in[0, at], edge_in[1, at]))
        field = without_halo(adjoint)
        pl.semaphore_wait(token.at[turn], 2)
        if turn == 0:
            signal(token.at[1], cells=along_z(2))
            signal(token.at[1], cells=along_z(-2))
        else:
            signal(token.at[2], ens=1 - ens)
        await_edges(pl.ds(1, 5) if turn == 0 else pl.ds(7, 1), turn * 2 + 1)
        low = edge_in[0, at + 1]
        high = edge_in[1, at + 1]
        for w in range(4):
            low = low - edge_in[0, 2 + w] * downward[:, w][:, None]
            high = high - edge_in[1, 2 + w] * upward[:, w][:, None]
        adjoint = apply_inverse(take_off(field, low, high))

    adj_ref[...] = adjoint
    for i in range(16):
        cell_grad = jnp.zeros((128, 128), F32)
        for m in range(2):
            for u in range(4):
                weight = jnp.broadcast_to(adj_ref[m, u, i // 8, i % 8 : i % 8 + 1], (128, 128))
                cell_grad = cell_grad + weight * turned[m * 4 + u, i].astype(F32)
        top = cell_grad.astype(BF16)
        rhs[:128, i * 128 : (i + 1) * 128] = top
        rhs[128:, i * 128 : (i + 1) * 128] = (cell_grad - top.astype(F32)).astype(BF16)
    def gather(rows):
        both = lax.dot_general(onehot[rows], rhs[...], (((1,), (1,)), ((), ())), preferred_element_type=F32)
        return (both[:, :128] + both[:, 128:]).reshape(8, 2, 16, 128)

    total[1] = gather(slice(256, 512))
    swap = remote(
        total.at[1], core_in, load_sem.at[2], core_sem,
        cells=cell + 1 - 2 * core,
    )
    swap.start()
    total[0] = gather(slice(0, 256))
    swap.wait_recv()
    for half in range(2):
        for step in range(8):
            mixed[half, step] = total[0, step, half] + core_in[step, half]
        for step in (6, 2, 5, 7, 1, 3, 4):
            remote(
                mixed.at[half, step], got.at[half, step - 1], load_sem.at[3], first_sem.at[half],
                cells=first_peer(step),
            ).start()
    pl.semaphore_wait(token.at[2], 1)
    own = ens * 8 + z
    for half in range(2):
        await_bytes(got.at[half], first_sem.at[half])
        partial = mixed[half, 0]
        for step in range(7):
            partial = partial + got[half, step]
        mine[half] = partial.reshape(4, 4, 128)
        for piece in ((2, 1, 3, 0), (0, 3, 1, 2))[half]:
            by = half * 4 + piece + 2
            for de in (1, 0):
                if by == 8 and de == 0:
                    arrived[own] = mine[half, piece]
                else:
                    remote(
                        mine.at[half, piece], arrived.at[own], load_sem.at[4], second_sem,
                        cells=along_z(by - 8), ens=(ens + de) % 2,
                    ).start()
    await_bytes(arrived.at[pl.ds(0, 15)], second_sem)
    gradient = arrived[0]
    for i in range(1, 16):
        gradient = gradient + arrived[i]
    grad_ref[...] = gradient

    @pl.when(has_above)
    def _():
        await_bytes(edge_out.at[0], load_sem.at[0])

    @pl.when(has_below)
    def _():
        await_bytes(edge_out.at[1], load_sem.at[1])

    swap.wait_send()
    await_bytes(got, load_sem.at[3])
    await_bytes(arrived.at[pl.ds(0, 15)], load_sem.at[4])


def writer(adj_ref, grad_ref, adj_out, grad_out, sem):
    copies = [
        pltpu.make_async_copy(src, dst, sem.at[i])
        for i, (src, dst) in enumerate([(adj_ref, adj_out), (grad_ref, grad_out)])
    ]
    for copy in copies:
        copy.start()
    for copy in copies:
        copy.wait()


def body(later_adjoint, coupling, diag_inverse, sensitivity, well_cells, well_misfit, block_map):
    any_spec = pl.BlockSpec(memory_space=pl.ANY)
    vmem = pl.BlockSpec(memory_space=pltpu.VMEM)
    args = (
        later_adjoint, coupling, diag_inverse, sensitivity.reshape(8, 16, 128, 128),
        well_cells.reshape(2, 128), well_misfit, block_map,
    )
    dma = pltpu.SemaphoreType.DMA
    adjoint, gradient = pl.pallas_call(
        kernel,
        out_shape=(pltpu.VMEM(later_adjoint.shape, F32), pltpu.VMEM((4, 128), F32)),
        in_specs=[any_spec] * 7,
        out_specs=(vmem, vmem),
        scratch_shapes=[pltpu.VMEM(a.shape, a.dtype) for a in args] + [
            pltpu.VMEM((8, 16, 128, 128), BF16),
            pltpu.VMEM((512, 2048), BF16),
            pltpu.VMEM((256, 2048), BF16),
            pltpu.VMEM((2, 8, 2, 16, 128), F32),
            pltpu.VMEM((8, 2, 16, 128), F32),
            pltpu.VMEM((2, 8, 16, 128), F32),
            pltpu.VMEM((2, 7, 16, 128), F32),
            pltpu.VMEM((2, 4, 4, 128), F32),
            pltpu.VMEM((16, 4, 128), F32),
            pltpu.VMEM((2, 8, 2, 4, 8, 128), F32),
            pltpu.VMEM((2, 8, 2, 4, 8, 128), F32),
            dma((7,)), dma((2, 4)), dma(()), dma((2,)), dma(()),
            pltpu.SemaphoreType.REGULAR((3,)),
        ],
        compiler_params=pltpu.CompilerParams(collective_id=0, has_side_effects=True),
        name="adjoint_step",
    )(*args)
    return pl.pallas_call(
        writer,
        out_shape=(
            jax.ShapeDtypeStruct(adjoint.shape, F32),
            jax.ShapeDtypeStruct(gradient.shape, F32),
        ),
        in_specs=[any_spec, any_spec],
        out_specs=(any_spec, any_spec),
        scratch_shapes=[dma((2,))],
        name="write_out",
    )(*(pltpu.with_memory_space_constraint(a, pltpu.VMEM) for a in (adjoint, gradient)))


def solution(mesh):
    placed = (
        P("ens", None, "cells", None, None),
        P("ens", None, None, None, "cells", None, None),
        P("ens", None, None, "cells", None, None),
        P("ens", None, "cells", None, None, None),
        P(),
        P("ens", None, None),
        P("cells", None, None),
    )
    return jax.shard_map(
        body,
        mesh=mesh,
        in_specs=placed,
        out_specs=(P("ens", None, "cells", None, None), P("cells", None)),
        check_vma=False,
    )
```

time: 44 us -> 31.7 us (0.72)
  Pallas kernels: 40.2 us -> 30.9 us
  local copies, waits for them, and re-layouts: 2.72 us -> 0 us
    pallas_call x1 -> x2, Pallas kernels: 40.2 us -> 30.9 us  [the longest x1 30.2 us: body(): pl.pallas_call(kernel, out_shape=(pltpu.VMEM(later_adjoint.shape, F32), p...]
    unnamed x2 -> x0, local copies, waits for them, and re-layouts: 2.72 us -> none
where the time goes in v2:
time: 31.7 us; the launch traced here: 31.5 us
  Pallas kernels  30.9 us (97%)
  between operations  0.64 us (2%)
    pallas_call x1, Pallas kernels, body(): pl.pallas_call(kernel, out_shape=(pltpu.VMEM(later_adjoint.shape, F32), p...  30.2 us
    pallas_call x1, Pallas kernels, body(): pl.pallas_call(writer, out_shape=(jax.ShapeDtypeStruct(adjoint.shape, F32...  0.65 us

profile of v2, /device:TPU:1, one launch (start us, length us, event | category | flops | bytes accessed | tf_op | source)
XLA Modules:
  0.0 31.5 jit_solution(10033651868830312136)
XLA Ops:
  0.6 30.2 %adjoint_step.1 = (f32[2,4,2,8,128]{4,3,2,1,0:T(8,128)S(1)}, f32[4,128]{1,0:T(4,128)S(1)}) custom-call(f32[2,4,2,8,128]{4,3,2,1,0:T(8,128)} %later_hbm.1, bf16[2,6,4,4,2,8,128]{6,5,4,3,2,1,0:T(8,128)(2,1)} %coup_hbm.1, bf16[2,4,4,2,8,128]{5,4,3,2,1,0:T(8,128)(2,1)} %dinv_hbm.1, bf16[8,16,128,128]{3,2,1,0:T(8,128)(2,1)} %bitcast.2, s32[2,128]{1,0:T(2,128)} %bitcast.3, ...), custom_call_target="tpu_custom_call" | custom-call | tf_op jit(solution)/shard_map/adjoint_step/pallas_call | solution.py:298
  30.9 0.7 %write_out.1 = (f32[2,4,2,8,128]{4,3,2,1,0:T(8,128)}, f32[4,128]{1,0:T(4,128)}) custom-call(f32[2,4,2,8,128]{4,3,2,1,0:T(8,128)S(1)} %get-tuple-element.4.adj_ref, f32[4,128]{1,0:T(4,128)S(1)} %get-tuple-element.5.grad_ref), custom_call_target="tpu_custom_call" | custom-call | tf_op jit(solution)/shard_map/write_out/pallas_call | solution.py:321
